TPU v7x, 32 devices: a whole 2x2x4 slice. The times are simulated.
32 devices in a mesh: unit: 4 (over z), bank: 4 (over x, core), zero: 2 (over y).
Axes of the slice: x: 2, y: 2, z: 4, core: 2. Of those that a mesh axis runs over, the one named last changes fastest.
Arguments:
- train_down: float32 [256, 1024, 2048], P(('unit', 'bank'), None, 'zero'), parts along dimension 0, may hold values from -0.25 to 0.25
- router_weight: float32 [8192, 64], P(('unit', 'zero'), 'bank'), parts along dimension 0, may hold values from -0.125 to 0.125
- router_gain: float32 [8192], P(('unit', 'zero')), parts along dimension 0, may hold values from 0.25 to 1.75
Outputs:
- ready_down: bfloat16 [256, 1024, 2048], P(('unit', 'bank'), 'zero'), parts along dimension 0
- scale_down: float32 [256, 1024], P(('unit', 'bank'), 'zero'), parts along dimension 0
- serve_router: bfloat16 [8192, 64], P('unit'), parts along dimension 0
There are 4 independent parts, one for each index of `unit`. A program takes and returns all parts, laid end to end along the dimension named above; each array names one. Nothing has to cross between parts.
All inputs are finite; a program needn't handle non-finite values.
Results may differ from a plain program's by a relative error of at most 0.001.
Values may be sent and summed in bfloat16 or wider, within the bound.
A program may use at most 256 MiB of HBM per device.

v0:
```python
import jax
import jax.numpy as jnp
from jax import lax
from jax.sharding import PartitionSpec as P


def per_device(train_down, router_weight, router_gain):
    scale_down = lax.pmax(jnp.max(jnp.abs(train_down), axis=2), "zero")
    narrow_down = (train_down / jnp.expand_dims(scale_down, 2)).astype(jnp.bfloat16)
    ready_down = lax.all_to_all(narrow_down, "zero", split_axis=1, concat_axis=2, tiled=True)
    scale_down = lax.dynamic_slice_in_dim(
        scale_down, lax.axis_index("zero") * ready_down.shape[1], ready_down.shape[1], axis=1
    )
    part_router = (router_weight * router_gain[:, None]).astype(jnp.bfloat16)
    row_router = lax.all_gather(part_router, "zero", axis=0, tiled=True)
    serve_router = lax.all_gather(row_router, "bank", axis=1, tiled=True)
    return (ready_down, scale_down, serve_router)


def solution(mesh):
    in_specs = (P(("unit", "bank"), None, "zero"), P(("unit", "zero"), "bank"), P(("unit", "zero")))
    out_specs = (P(("unit", "bank"), "zero", None), P(("unit", "bank"), "zero"), P("unit", None))
    return jax.shard_map(
        per_device, mesh=mesh, in_specs=in_specs, out_specs=out_specs, check_vma=False
    )
```

profile of v0, /device:TPU:0, one launch (start us, length us, event | category | flops | bytes accessed | tf_op | source)
XLA Modules:
  0.0 617.8 jit_solution(3817814109771987231)
XLA Ops:
  7.2 0.0 all-reduce.2.cloned.1.call-start
  7.2 21.4 %abs_reduce_fusion = f32[16,1024]{1,0:T(8,128)} fusion(f32[16,1024,1024]{2,1,0:T(8,128)} %param.3), kind=kLoop, calls=%fused_computation.2 | loop fusion | flops 33538048 | bytes 67174400 | tf_op jit(solution)/shard_map/reduce_max | solution.py:8
  28.6 0.0 all-reduce.2.cloned.1.call-update
  28.6 23.8 %all-reduce.2.cloned.1.call-done = f32[16,1024]{1,0:T(8,128)} async-done(((f32[16,1024]{1,0:T(8,128)}), f32[16,1024]{1,0:T(8,128)}) %all-reduce.2.cloned.1.call-update) | async-done | bytes 65552 | tf_op jit(solution)/shard_map/pmax | solution.py:8
  52.5 1.0 copy.7
  53.5 0.0 copy-start.1
  53.5 0.0 copy-start.2
  53.6 0.0 copy-start
  53.6 60.1 %fusion = bf16[16,1024,1024]{2,0,1:T(8,128)(2,1)} fusion(f32[16,1024,1024]{2,1,0:T(8,128)} %param.3, f32[16,1024]{0,1:T(8,128)S(1)} %copy.7), kind=kLoop, calls=%fused_computation.1 | loop fusion | flops 33554432 | bytes 100728832 | tf_op jit(solution)/shard_map/convert_element_type | solution.py:9
  113.7 13.0 %all-to-all-start = ((bf16[16,1024,1024]{2,0,1:T(8,128)(2,1)}), bf16[16,1024,1024]{2,0,1:T(8,128)(2,1)}, u32[]{:S(2)}, u32[]{:S(2)}) async-start(bf16[16,1024,1024]{2,0,1:T(8,128)(2,1)} %fusion), calls=%async_computation | async-start | bytes 67108864 | tf_op jit(solution)/shard_map/all_to_all | solution.py:10
  126.7 0.0 copy-done.1
  126.7 0.0 copy-done.2
  126.7 362.4 %all_gather.6 = bf16[2048,16]{0,1:T(8,128)(2,1)S(1)} all-gather(bf16[1024,16]{0,1:T(8,128)(2,1)S(1)} %multiply_convert_fusion), channel_id=1, replica_groups=mesh['unit'=4,'bank'=4,'zero'=2] {'zero'}, dimensions={0}, use_global_device_ids=true | all-gather | bytes 98304 | tf_op jit(solution)/shard_map/all_gather | solution.py:15
  489.1 5.8 all_gather.7
  494.8 0.0 copy-done
  494.8 0.6 constant_dynamic-slice_fusion
  495.5 0.0 all-to-all-done
  495.5 60.5 %copy.9 = bf16[16,512,2,1024]{3,2,1,0:T(2,128)(2,1)} copy(bf16[16,512,2,1024]{3,0,1,2:T(8,128)(2,1)} %bitcast.1) | data formatting | bytes 67108864 | tf_op jit(solution)/shard_map/all_to_all | solution.py:10
  556.0 54.2 %all_to_all.16 = bf16[16,512,2048]{2,1,0:T(8,128)(2,1)} reshape(bf16[16,512,2,1024]{3,2,1,0:T(2,128)(2,1)} %copy.9) | data formatting | bytes 67108864 | tf_op jit(solution)/shard_map/all_to_all | solution.py:10
  610.2 0.7 copy.15
  (1 shorter events, 0.0 us)
Async XLA Ops:
  7.2 45.3 %all-reduce.2.cloned.1.call-start = ((), (), s32[]{:S(2)}) async-start(), calls=%async_computation.1 | async-start | bytes 131072 | tf_op jit(solution)/shard_map/pmax | solution.py:8
  53.5 73.1 %copy-start.1 = (f32[1024,16]{0,1:T(8,128)S(1)}, f32[1024,16]{0,1:T(8,128)}, u32[]{:S(2)}) copy-start(f32[1024,16]{0,1:T(8,128)} %param.4) | copy-start | bytes 196612
  53.5 73.1 %copy-start.2 = (f32[1024]{0:T(1024)S(1)}, f32[1024]{0:T(1024)}, u32[]{:S(2)}) copy-start(f32[1024]{0:T(1024)} %param.5) | copy-start | bytes 12292
  53.6 441.3 %copy-start = (f32[16,1024]{1,0:T(8,128)S(1)}, f32[16,1024]{1,0:T(8,128)}, u32[]{:S(2)}) copy-start(f32[16,1024]{1,0:T(8,128)} %all-reduce.2.cloned.1.call-done) | copy-start | bytes 196612
  113.7 381.8 %all-to-all-start = ((bf16[16,1024,1024]{2,0,1:T(8,128)(2,1)}), bf16[16,1024,1024]{2,0,1:T(8,128)(2,1)}, u32[]{:S(2)}, u32[]{:S(2)}) async-start(bf16[16,1024,1024]{2,0,1:T(8,128)(2,1)} %fusion), calls=%async_computation | async-start | bytes 67108864 | tf_op jit(solution)/shard_map/all_to_all | solution.py:10
Sparse Core Ops, SparseCore 0:
  28.8 23.6 all-reduce.1
where the time goes:
time: 619 us; the launch traced here: 618 us
  blocking collectives  368 us (59%)
  local copies, waits for them, and re-layouts  117 us (19%)
  other arithmetic  81.6 us (13%)
  waiting for transfers between devices  23.9 us (4%)
  between operations  14.1 us (2%)
  starting transfers between devices  13 us (2%)
    all_gather x1, blocking collectives, per_device(): row_router = lax.all_gather(part_router, 'zero', axis=0, tiled=True)  362 us
    all_to_all x2, local copies, waits for them, and re-layouts, per_device(): lax.all_to_all(narrow_down, 'zero', split_axis=1, concat_axis=2, tiled=True)  115 us
    convert_element_type x1, other arithmetic, per_device(): (train_down / jnp.expand_dims(scale_down, 2)).astype(jnp.bfloat16)  60.1 us
    pmax x1, waiting for transfers between devices, per_device(): scale_down = lax.pmax(jnp.max(jnp.abs(train_down), axis=2), 'zero')  23.8 us
    reduce_max x1, other arithmetic, per_device(): scale_down = lax.pmax(jnp.max(jnp.abs(train_down), axis=2), 'zero')  21.4 us
    all_to_all x1, starting transfers between devices, per_device(): lax.all_to_all(narrow_down, 'zero', split_axis=1, concat_axis=2, tiled=True)  13 us
  transfers between devices with their start and end apart: 2, of which 1 were waited for; matrix products, arithmetic and copies ran while one was open for 0% of the time, Pallas kernels for 0%

commit v1 on v0

--- a/solution.py
+++ b/solution.py
@@ -7,7 +7,12 @@
 def per_device(train_down, router_weight, router_gain):
     scale_down = lax.pmax(jnp.max(jnp.abs(train_down), axis=2), "zero")
     narrow_down = (train_down / jnp.expand_dims(scale_down, 2)).astype(jnp.bfloat16)
-    ready_down = lax.all_to_all(narrow_down, "zero", split_axis=1, concat_axis=2, tiled=True)
+    ready_down = jnp.concatenate(
+        lax.all_to_all(
+            jnp.stack(jnp.split(narrow_down, lax.axis_size("zero"), axis=1)), "zero", 0, 0
+        ),
+        axis=2,
+    )
     scale_down = lax.dynamic_slice_in_dim(
         scale_down, lax.axis_index("zero") * ready_down.shape[1], ready_down.shape[1], axis=1
     )

time: 619 us -> 544 us (0.88)
  local copies, waits for them, and re-layouts: 117 us -> 47.7 us
    all_to_all x2 -> x0, local copies, waits for them, and re-layouts: 115 us -> none  [per_device(): lax.all_to_all(narrow_down, 'zero', split_axis=1, concat_axis=2, tiled=True)]
    convert_element_type x1, other arithmetic: 60.1 us -> 32.9 us  [per_device(): (train_down / jnp.expand_dims(scale_down, 2)).astype(jnp.bfloat16)]
    reshape x0 -> x1, local copies, waits for them, and re-layouts: none -> 23.3 us  [per_device(): jnp.concatenate(lax.all_to_all(jnp.stack(jnp.split(narrow_down, lax.axis_...]
    another operation x0 -> x1, local copies, waits for them, and re-layouts: none -> 23.1 us  [per_device(): jnp.stack(jnp.split(narrow_down, lax.axis_size('zero'), axis=1))]
    another operation x0 -> x1, other arithmetic: none -> 23 us  [per_device(): jnp.stack(jnp.split(narrow_down, lax.axis_size('zero'), axis=1))]
where the time goes in v1:
time: 544 us
  blocking collectives  368 us (68%)
  other arithmetic  77.3 us (14%)
  local copies, waits for them, and re-layouts  47.7 us (9%)
  waiting for transfers between devices  23.9 us (4%)
  between operations  14.1 us (3%)
  starting transfers between devices  13.1 us (2%)
    all_gather x1, blocking collectives, per_device(): row_router = lax.all_gather(part_router, 'zero', axis=0, tiled=True)  362 us
    convert_element_type x1, other arithmetic, per_device(): (train_down / jnp.expand_dims(scale_down, 2)).astype(jnp.bfloat16)  32.9 us
    pmax x1, waiting for transfers between devices, per_device(): scale_down = lax.pmax(jnp.max(jnp.abs(train_down), axis=2), 'zero')  23.8 us
    reshape x1, local copies, waits for them, and re-layouts, per_device(): jnp.concatenate(lax.all_to_all(jnp.stack(jnp.split(narrow_down, lax.axis_...  23.3 us
    another operation x1, local copies, waits for them, and re-layouts, per_device(): jnp.stack(jnp.split(narrow_down, lax.axis_size('zero'), axis=1))  23.1 us
    another operation x1, other arithmetic, per_device(): jnp.stack(jnp.split(narrow_down, lax.axis_size('zero'), axis=1))  23 us
    reduce_max x1, other arithmetic, per_device(): scale_down = lax.pmax(jnp.max(jnp.abs(train_down), axis=2), 'zero')  21.4 us
    all_to_all x1, starting transfers between devices, per_device(): lax.all_to_all(jnp.stack(jnp.split(narrow_down, lax.axis_size('zero'), ax...  13.1 us
  transfers between devices with their start and end apart: 2, of which 1 were waited for; matrix products, arithmetic and copies ran while one was open for 0% of the time, Pallas kernels for 0%

profile of v1, /device:TPU:0, one launch (start us, length us, event | category | flops | bytes accessed | tf_op | source)
XLA Modules:
  0.0 544.2 jit_solution(9817326848428863188)
XLA Ops:
  7.2 0.0 all-reduce.2.cloned.1.call-start
  7.2 21.4 %abs_reduce_fusion = f32[16,1024]{1,0:T(8,128)} fusion(f32[16,1024,1024]{2,1,0:T(8,128)} %param.3), kind=kLoop, calls=%fused_computation.1 | loop fusion | flops 33538048 | bytes 67174400 | tf_op jit(solution)/shard_map/reduce_max | solution.py:8
  28.6 0.0 all-reduce.2.cloned.1.call-update
  28.6 23.8 %all-reduce.2.cloned.1.call-done = f32[16,1024]{1,0:T(8,128)} async-done(((f32[16,1024]{1,0:T(8,128)}), f32[16,1024]{1,0:T(8,128)}) %all-reduce.2.cloned.1.call-update) | async-done | bytes 65552 | tf_op jit(solution)/shard_map/pmax | solution.py:8
  52.5 32.9 %divide_convert_fusion = bf16[16,1024,1024]{2,1,0:T(8,128)(2,1)} fusion(f32[16,1024,1024]{2,1,0:T(8,128)} %param.3, f32[16,1024]{1,0:T(8,128)} %all-reduce.2.cloned.1.call-done), kind=kLoop, calls=%fused_computation | loop fusion | flops 33554432 | bytes 100728832 | tf_op jit(solution)/shard_map/convert_element_type | solution.py:9
  85.4 23.1 %slice_bitcast_fusion.1 = (bf16[1,16,512,1024]{3,2,1,0:T(8,128)(2,1)}, bf16[1,16,512,1024]{3,2,1,0:T(8,128)(2,1)}) fusion(bf16[16,1024,1024]{2,1,0:T(8,128)(2,1)} %divide_convert_fusion), kind=kLoop, calls=%fused_computation.4 | loop fusion | bytes 67108864 | tf_op jit(solution)/shard_map/stack | solution.py:12
  108.5 23.0 %pad_maximum_fusion = bf16[2,16,512,1024]{3,2,1,0:T(8,128)(2,1)} fusion(bf16[1,16,512,1024]{3,2,1,0:T(8,128)(2,1)} %get-tuple-element.4, bf16[1,16,512,1024]{3,2,1,0:T(8,128)(2,1)} %get-tuple-element.3), kind=kLoop, calls=%fused_computation.2 | loop fusion | flops 16777216 | bytes 67108864 | tf_op jit(solution)/shard_map/stack | solution.py:12
  131.4 0.0 copy-start.1
  131.5 0.0 copy-start.2
  131.5 0.0 copy-start
  131.5 13.1 %all-to-all-start = ((bf16[2,16,512,1024]{3,2,1,0:T(8,128)(2,1)}), bf16[2,16,512,1024]{3,2,1,0:T(8,128)(2,1)}, u32[]{:S(2)}, u32[]{:S(2)}) async-start(bf16[2,16,512,1024]{3,2,1,0:T(8,128)(2,1)} %pad_maximum_fusion), calls=%async_computation | async-start | bytes 67108864 | tf_op jit(solution)/shard_map/all_to_all | solution.py:11
  144.6 0.0 copy-done.1
  144.6 0.0 copy-done.2
  144.6 362.4 %all_gather.6 = bf16[2048,16]{0,1:T(8,128)(2,1)S(1)} all-gather(bf16[1024,16]{0,1:T(8,128)(2,1)S(1)} %multiply_convert_fusion), channel_id=1, replica_groups=mesh['unit'=4,'bank'=4,'zero'=2] {'zero'}, dimensions={0}, use_global_device_ids=true | all-gather | bytes 98304 | tf_op jit(solution)/shard_map/all_gather | solution.py:20
  507.0 5.8 %all_gather.7 = bf16[2048,64]{0,1:T(8,128)(2,1)S(1)} all-gather(bf16[2048,16]{0,1:T(8,128)(2,1)S(1)} %all_gather.6), channel_id=1, replica_groups=mesh['unit'=4,'bank'=4,'zero'=2] {'bank'}, dimensions={1}, use_global_device_ids=true | all-gather | bytes 327680 | tf_op jit(solution)/shard_map/all_gather | solution.py:21
  512.8 0.0 copy-done
  512.8 0.6 constant_dynamic-slice_fusion
  513.4 0.0 all-to-all-done
  513.4 23.3 %copy.7 = bf16[2,16,64,8,1024]{4,3,0,2,1:T(8,128)(2,1)} copy(bf16[2,16,64,8,1024]{4,3,2,1,0:T(8,128)(2,1)} %bitcast.3) | data formatting | bytes 67108864 | tf_op jit(solution)/shard_map/reshape | solution.py:10
  536.7 0.7 copy.10
  (1 shorter events, 0.0 us)
Async XLA Ops:
  7.2 45.3 %all-reduce.2.cloned.1.call-start = ((), (), s32[]{:S(2)}) async-start(), calls=%async_computation.1 | async-start | bytes 131072 | tf_op jit(solution)/shard_map/pmax | solution.py:8
  131.4 13.2 %copy-start.1 = (f32[1024,16]{0,1:T(8,128)S(1)}, f32[1024,16]{0,1:T(8,128)}, u32[]{:S(2)}) copy-start(f32[1024,16]{0,1:T(8,128)} %param.4) | copy-start | bytes 196612
  131.5 13.2 %copy-start.2 = (f32[1024]{0:T(1024)S(1)}, f32[1024]{0:T(1024)}, u32[]{:S(2)}) copy-start(f32[1024]{0:T(1024)} %param.5) | copy-start | bytes 12292
  131.5 381.3 %copy-start = (f32[16,1024]{1,0:T(8,128)S(1)}, f32[16,1024]{1,0:T(8,128)}, u32[]{:S(2)}) copy-start(f32[16,1024]{1,0:T(8,128)} %all-reduce.2.cloned.1.call-done) | copy-start | bytes 196612
  131.5 381.9 %all-to-all-start = ((bf16[2,16,512,1024]{3,2,1,0:T(8,128)(2,1)}), bf16[2,16,512,1024]{3,2,1,0:T(8,128)(2,1)}, u32[]{:S(2)}, u32[]{:S(2)}) async-start(bf16[2,16,512,1024]{3,2,1,0:T(8,128)(2,1)} %pad_maximum_fusion), calls=%async_computation | async-start | bytes 67108864 | tf_op jit(solution)/shard_map/all_to_all | solution.py:11
Sparse Core Ops, SparseCore 0:
  28.8 23.6 all-reduce.1
